TPU v7x, 32 devices: a whole 2x2x4 slice. The times are simulated.
32 devices in a mesh: dp: 8 (over z, core), expert: 4 (over y, x).
Axes of the slice: x: 2, y: 2, z: 4, core: 2. Of those that a mesh axis runs over, the one named last changes fastest.
Arguments:
- mamba_in: bfloat16 [8, 256, 4096], P('dp'), may hold values from -6 to 6
- conv_state: bfloat16 [8, 3, 8192], P('dp', None, 'expert'), may hold values from -6 to 6
- in_weight: bfloat16 [4096, 8192], P('dp', 'expert'), may hold values from -0.09375 to 0.09375
- conv_kernel: float32 [4, 8192], P(None, 'expert'), may hold values from -3 to 3
- conv_bias: float32 [8192], P('expert'), may hold values from -1 to 1
- moe_in: bfloat16 [512, 4096], P('expert'), may hold values from -6 to 6
- router: bfloat16 [4096, 4], replicated, may hold values from -0.09375 to 0.09375
- expert_ids: int32 [512, 2], P('expert'), may hold values from 0 to 3, all different within a row; in each aligned block of 128 rows (0 to 127, 128 to 255, ...) at most 128 rows name the same one
- w_gate: bfloat16 [4, 4096, 12288], P('expert', None, 'dp'), may hold values from -0.09375 to 0.09375
- w_up: bfloat16 [4, 4096, 12288], P('expert', None, 'dp'), may hold values from -0.09375 to 0.09375
- w_down: bfloat16 [4, 12288, 4096], P('expert', 'dp'), may hold values from -0.078125 to 0.078125
Outputs:
- conv_out: bfloat16 [8, 256, 8192], P('dp', None, 'expert')
- moe_out: bfloat16 [512, 4096], P('expert', 'dp')
Inputs may be any that keep to these rules, and one draw needn't show every extreme that they name: `expert_ids`: each row names two different experts; among the 128 rows of one index of expert no expert is named more than 128 times, a bound that some block reaches.
All inputs are finite; a program needn't handle non-finite values.
Results may differ from a plain program's by a relative error of at most 0.0049.
Values may be sent and summed in bfloat16 or wider, within the bound.
No kernel may reach another device: no remote copies, remote signals or barrier semaphores. Data moves between devices by JAX's collectives and lax.ppermute only.
A program may use at most 192 MiB of HBM per device.

v0:
```python
import jax
import jax.numpy as jnp
from jax import lax
from jax.sharding import PartitionSpec as P


def expert_ffn(inputs, gate_mat, up_mat, down_mat):
    gate_val = jnp.dot(inputs, gate_mat, preferred_element_type=jnp.float32)
    up_val = jnp.dot(inputs, up_mat, preferred_element_type=jnp.float32)
    hidden = (jax.nn.silu(gate_val) * up_val).astype(jnp.bfloat16)
    return jnp.dot(hidden, down_mat, preferred_element_type=jnp.float32)


def body(
    mamba_in,
    conv_state,
    in_weight,
    conv_kernel,
    conv_bias,
    moe_in,
    router,
    expert_ids,
    w_gate,
    w_up,
    w_down,
):
    token_count = mamba_in.shape[1]
    width = mamba_in.shape[2]
    window = mamba_in.reshape(token_count, width)
    channels = in_weight.shape[1]
    taps = conv_kernel.shape[0]
    summed_proj = jnp.dot(
        window,
        lax.all_gather(in_weight, "dp", axis=0, tiled=True),
        preferred_element_type=jnp.float32,
    )
    projected = summed_proj.astype(jnp.bfloat16)
    extended = jnp.concatenate([conv_state[0], projected], axis=0)
    summed = jnp.zeros((token_count, channels), jnp.float32) + conv_bias[None, :]
    for offset in range(taps):
        summed = (
            summed
            + extended[offset : offset + token_count].astype(jnp.float32)
            * conv_kernel[offset][None, :]
        )
    conv_out = jax.nn.silu(summed).astype(jnp.bfloat16).reshape(1, token_count, channels)
    moe_rows = moe_in.shape[0]
    experts = lax.axis_size("expert") * w_gate.shape[0]
    capacity = min(moe_rows, 4 * moe_rows // experts)
    expert_range = jnp.arange(experts, dtype=jnp.int32)
    onehot_ids = (expert_ids.reshape(-1)[:, None] == expert_range[None, :]).astype(jnp.int32)
    earlier = jnp.cumsum(onehot_ids, axis=0) - onehot_ids
    slots = jnp.sum(earlier * onehot_ids, axis=1).reshape(moe_rows, 2)
    targets = expert_ids * capacity + slots
    slot_range = jnp.arange(experts * capacity, dtype=jnp.int32)
    first_hit = targets[:, 0][None, :] == slot_range[:, None]
    second_hit = targets[:, 1][None, :] == slot_range[:, None]
    dispatch_table = jnp.logical_or(first_hit, second_hit).astype(jnp.bfloat16)
    send_buffer = jnp.dot(dispatch_table, moe_in, preferred_element_type=jnp.float32).astype(
        jnp.bfloat16
    )
    send_buffer = send_buffer.reshape(experts, capacity, width)
    logits = jnp.dot(moe_in, router, preferred_element_type=jnp.float32)
    chosen_mask = (expert_ids[:, :, None] == expert_range[None, None, :]).astype(jnp.float32)
    chosen = jnp.sum(logits[:, None, :] * chosen_mask, axis=2)
    first_weight = jax.nn.sigmoid(chosen[:, 0] - chosen[:, 1])
    combine_table = first_weight[:, None] * first_hit.T.astype(jnp.float32) + (1.0 - first_weight)[
        :, None
    ] * second_hit.T.astype(jnp.float32)
    received = lax.all_to_all(send_buffer, "expert", split_axis=0, concat_axis=0, tiled=True)
    flat_rows = received.reshape(-1, width)
    result = expert_ffn(flat_rows, w_gate[0], w_up[0], w_down[0])
    partials = result.reshape(received.shape[0], received.shape[1], width)
    shares = lax.psum_scatter(partials, "dp", scatter_dimension=2, tiled=True)
    returned = lax.all_to_all(shares, "expert", split_axis=0, concat_axis=0, tiled=True)
    flat_back = returned.reshape(experts * capacity, returned.shape[2])
    mixed = jnp.dot(
        combine_table,
        flat_back,
        precision=lax.Precision.HIGHEST,
        preferred_element_type=jnp.float32,
    )
    return (conv_out, mixed.astype(jnp.bfloat16))


def solution(mesh):
    in_specs = (
        P("dp", None, None),
        P("dp", None, "expert"),
        P("dp", "expert"),
        P(None, "expert"),
        P("expert"),
        P("expert", None),
        P(),
        P("expert", None),
        P("expert", None, "dp"),
        P("expert", None, "dp"),
        P("expert", "dp", None),
    )
    out_specs = (P("dp", None, "expert"), P("expert", "dp"))
    return jax.shard_map(body, mesh=mesh, in_specs=in_specs, out_specs=out_specs, check_vma=False)
```

profile of v0, /device:TPU:0, one launch (start us, length us, event | category | flops | bytes accessed | tf_op | source)
XLA Modules:
  0.0 353.5 jit_solution(8871153900584539604)
XLA Ops:
  7.2 0.0 copy-start
  7.2 0.0 reduce-scatter.2.cloned.1.call-start
  7.2 0.9 copy.39
  8.2 0.1 eq.86
  8.3 0.1 eq.82
  8.4 1.2 reduce-window.6
  9.7 0.1 slice.56
  9.7 0.1 copy.41
  9.9 0.1 copy.42
  10.0 0.1 add_bitcast_fusion
  10.1 0.1 reshape.49
  10.2 0.1 copy.43
  10.3 0.7 multiply_add_fusion
  11.0 0.0 copy-start.6
  11.0 2.6 convolution_convert_fusion
  13.6 0.0 slice-start
  13.6 53.1 %all_to_all.10 = bf16[4,128,4096]{2,1,0:T(8,128)(2,1)S(1)} all-to-all(bf16[4,128,4096]{2,1,0:T(8,128)(2,1)S(1)} %bitcast.62), channel_id=1, replica_groups=mesh['dp'=8,'expert'=4] {'expert'}, dimensions={0} | all-to-all | bytes 8388608 | tf_op jit(solution)/shard_map/all_to_all | solution.py:70
  66.7 0.0 copy-done.6
  66.7 0.0 slice-start.1
  66.7 0.0 slice-start.2
  66.7 8.3 %fusion.4 = f32[512,1536]{1,0:T(8,128)} fusion(bf16[512,4096]{1,0:T(8,128)(2,1)S(1)} %bitcast.63, bf16[1,4096,1536]{2,1,0:T(8,128)(2,1)S(1)} %copy-done.6), kind=kOutput, calls=%fused_computation.4 | convolution fusion | flops 6442450944 | bytes 19922944 | tf_op jit(solution)/shard_map/dot_general | solution.py:8
  75.0 0.0 slice-done
  75.0 0.0 slice-done.1
  75.0 0.0 slice-done.2
  75.0 8.5 %fusion.9 = bf16[512,1536]{1,0:T(8,128)(2,1)S(1)} fusion(bf16[512,4096]{1,0:T(8,128)(2,1)S(1)} %bitcast.64, bf16[1,4096,1536]{2,1,0:T(8,128)(2,1)S(1)} %bitcast.74, f32[512,1536]{1,0:T(8,128)} %fusion.4), kind=kOutput, calls=%fused_computation.8 | convolution fusion | flops 6447169536 | bytes 21495808 | tf_op jit(solution)/shard_map/dot_general | solution.py:9
  83.5 11.8 %fusion = f32[4,128,4096]{2,1,0:T(8,128)} fusion(bf16[4,128,1536]{2,1,0:T(8,128)(2,1)S(1)} %bitcast.75, bf16[1,1536,4096]{2,1,0:T(8,128)(2,1)} %param.21), kind=kOutput, calls=%fused_computation | convolution fusion | flops 6442450944 | bytes 22544384 | tf_op jit(solution)/shard_map/dot_general | solution.py:11
  95.3 0.0 reduce-scatter.2.cloned.1.call-update
  95.4 0.0 copy-start.1
  95.4 0.0 all-gather.2.cloned.1.call-start
  95.4 0.7 all-gather.2.cloned.1.call-update
  96.1 0.0 copy-start.4
  96.1 0.0 copy-start.2
  96.2 88.7 %reduce-scatter.2.cloned.1.call-done = f32[4,128,512]{2,1,0:T(8,128)} async-done(((f32[4,128,4096]{2,1,0:T(8,128)}), f32[4,128,512]{2,1,0:T(8,128)}) %reduce-scatter.2.cloned.1.call-update) | async-done | bytes 1048592 | tf_op jit(solution)/shard_map/reduce_scatter | solution.py:74
  184.8 3.7 %all-to-all-start.1 = ((f32[4,128,512]{2,1,0:T(8,128)}), f32[4,128,512]{2,1,0:T(8,128)S(1)}, u32[]{:S(2)}, u32[]{:S(2)}) async-start(f32[4,128,512]{2,1,0:T(8,128)} %reduce-scatter.2.cloned.1.call-done), calls=%async_computation.2 | async-start | bytes 2097152 | tf_op jit(solution)/shard_map/all_to_all | solution.py:75
  188.5 0.0 copy-done.1
  188.6 1.6 fusion.33
  190.2 0.0 copy-done.4
  190.2 0.0 copy-done.2
  190.2 9.9 %all-to-all-done.1 = f32[4,128,512]{2,1,0:T(8,128)S(1)} async-done(((f32[4,128,512]{2,1,0:T(8,128)}), f32[4,128,512]{2,1,0:T(8,128)S(1)}, u32[]{:S(2)}, u32[]{:S(2)}) %all-to-all-start.1) | async-done | bytes 1048608 | tf_op jit(solution)/shard_map/all_to_all | solution.py:75
  200.1 1.4 convolution_convert_fusion.2
  201.5 0.0 copy-start.3
  201.5 0.0 copy-start.5
  201.5 134.5 %all-gather.2.cloned.1.call-done = bf16[4096,2048]{1,0:T(8,128)(2,1)} async-done(((bf16[512,2048]{1,0:T(8,128)(2,1)}), bf16[4096,2048]{1,0:T(8,128)(2,1)}) %all-gather.2.cloned.1.call-update) | async-done | bytes 16777232 | tf_op jit(solution)/shard_map/all_gather | solution.py:34
  336.0 0.0 copy-done
  336.0 8.3 %convolution_convert_fusion.1 = bf16[256,2048]{1,0:T(8,128)(2,1)S(1)} fusion(bf16[4096,2048]{1,0:T(8,128)(2,1)} %all-gather.2.cloned.1.call-done, bf16[1,256,4096]{2,1,0:T(8,128)(2,1)S(1)} %copy-done), kind=kOutput, calls=%fused_computation.9 | convolution fusion | flops 4295491584 | bytes 19922944 | tf_op jit(solution)/shard_map/dot_general | solution.py:32
  344.3 0.0 copy-done.3
  344.3 0.0 copy-done.5
  344.3 2.3 fusion.15
  (9 shorter events, 0.1 us)
Async XLA Ops:
  7.2 328.8 %copy-start = (bf16[1,256,4096]{2,1,0:T(8,128)(2,1)S(1)}, bf16[1,256,4096]{2,1,0:T(8,128)(2,1)}, u32[]{:S(2)}) copy-start(bf16[1,256,4096]{2,1,0:T(8,128)(2,1)} %param.11) | copy-start | bytes 6291460
  7.2 177.7 %reduce-scatter.2.cloned.1.call-start = ((), (), s32[]{:S(2)}) async-start(), calls=%async_computation.4 | async-start | bytes 9437184 | tf_op jit(solution)/shard_map/reduce_scatter | solution.py:74
  11.0 55.7 %copy-start.6 = (bf16[1,4096,1536]{2,1,0:T(8,128)(2,1)S(1)}, bf16[1,4096,1536]{2,1,0:T(8,128)(2,1)}, u32[]{:S(2)}) copy-start(bf16[1,4096,1536]{2,1,0:T(8,128)(2,1)} %param.19) | copy-start | bytes 37748740
  13.6 61.4 %slice-start = ((s8[12582912]{0:T(1024)(128)(4,1)}), s8[4194304]{0:T(1024)(128)(4,1)S(1)}, s32[]{:S(2)}) async-start(s8[12582912]{0:T(1024)(128)(4,1)} %bitcast.73), calls=%async_computation.5 | async-start | bytes 8388608
  66.7 8.3 %slice-start.1 = ((s8[12582912]{0:T(1024)(128)(4,1)}), s8[4194304]{0:T(1024)(128)(4,1)S(1)}, s32[]{:S(2)}) async-start(s8[12582912]{0:T(1024)(128)(4,1)} %bitcast.73), calls=%async_computation.6 | async-start | bytes 8388608
  66.7 8.3 %slice-start.2 = ((s8[12582912]{0:T(1024)(128)(4,1)}), s8[4194304]{0:T(1024)(128)(4,1)S(1)}, s32[]{:S(2)}) async-start(s8[12582912]{0:T(1024)(128)(4,1)} %bitcast.73), calls=%async_computation.7 | async-start | bytes 8388608
  95.4 93.2 %copy-start.1 = (bf16[4096,4]{0,1:T(4,128)(2,1)S(1)}, bf16[4096,4]{0,1:T(4,128)(2,1)}, u32[]{:S(2)}) copy-start(bf16[4096,4]{0,1:T(4,128)(2,1)} %param.17) | copy-start | bytes 98308
  95.4 240.6 %all-gather.2.cloned.1.call-start = ((), (), s32[]{:S(2)}) async-start(), calls=%async_computation.3 | async-start | bytes 18874368 | tf_op jit(solution)/shard_map/all_gather | solution.py:34
  96.1 94.0 %copy-start.4 = (s32[128,2]{0,1:T(2,128)S(1)}, s32[128,2]{0,1:T(2,128)}, u32[]{:S(2)}) copy-start(s32[128,2]{0,1:T(2,128)} %param.18) | copy-start | bytes 3076
  96.1 94.1 %copy-start.2 = (f32[4,2048]{1,0:T(4,128)S(1)}, f32[4,2048]{1,0:T(4,128)}, u32[]{:S(2)}) copy-start(f32[4,2048]{1,0:T(4,128)} %param.14) | copy-start | bytes 98308
  184.8 15.3 %all-to-all-start.1 = ((f32[4,128,512]{2,1,0:T(8,128)}), f32[4,128,512]{2,1,0:T(8,128)S(1)}, u32[]{:S(2)}, u32[]{:S(2)}) async-start(f32[4,128,512]{2,1,0:T(8,128)} %reduce-scatter.2.cloned.1.call-done), calls=%async_computation.2 | async-start | bytes 2097152 | tf_op jit(solution)/shard_map/all_to_all | solution.py:75
  201.5 142.7 %copy-start.3 = (bf16[1,3,2048]{2,1,0:T(4,128)(2,1)S(1)}, bf16[1,3,2048]{2,1,0:T(4,128)(2,1)}, u32[]{:S(2)}) copy-start(bf16[1,3,2048]{2,1,0:T(4,128)(2,1)} %param.12) | copy-start | bytes 36868
  201.5 142.7 %copy-start.5 = (f32[2048]{0:T(1024)S(1)}, f32[2048]{0:T(1024)}, u32[]{:S(2)}) copy-start(f32[2048]{0:T(1024)} %param.15) | copy-start | bytes 24580
Sparse Core Ops, SparseCore 0:
  95.5 89.3 reduce-scatter.1
  186.4 149.5 all-gather.1
where the time goes:
time: 354 us; the launch traced here: 353 us
  waiting for transfers between devices  234 us (66%)
  blocking collectives  53.1 us (15%)
  matrix products  42.5 us (12%)
  between operations  14.2 us (4%)
  other arithmetic  4.44 us (1%)
  starting transfers between devices  3.77 us (1%)
    all_gather x1, waiting for transfers between devices, body(): lax.all_gather(in_weight, 'dp', axis=0, tiled=True)  134 us
    reduce_scatter x1, waiting for transfers between devices, body(): shares = lax.psum_scatter(partials, 'dp', scatter_dimension=2, tiled=True)  88.7 us
    all_to_all x1, blocking collectives, body(): lax.all_to_all(send_buffer, 'expert', split_axis=0, concat_axis=0, tiled=...  53.1 us
    dot_general x1, matrix products, expert_ffn(): return jnp.dot(hidden, down_mat, preferred_element_type=jnp.float32)  11.8 us
    all_to_all x1, waiting for transfers between devices, body(): lax.all_to_all(shares, 'expert', split_axis=0, concat_axis=0, tiled=True)  9.86 us
    dot_general x1, matrix products, expert_ffn(): up_val = jnp.dot(inputs, up_mat, preferred_element_type=jnp.float32)  8.53 us
    dot_general x1, matrix products, expert_ffn(): gate_val = jnp.dot(inputs, gate_mat, preferred_element_type=jnp.float32)  8.28 us
    dot_general x1, matrix products, body(): jnp.dot(window, lax.all_gather(in_weight, 'dp', axis=0, tiled=True), pref...  8.25 us
  transfers between devices with their start and end apart: 3, of which 3 were waited for; matrix products, arithmetic and copies ran while one was open for 1% of the time, Pallas kernels for 0%

commit v1 on v0

--- a/solution.py
+++ b/solution.py
@@ -2,6 +2,27 @@
 import jax.numpy as jnp
 from jax import lax
 from jax.sharding import PartitionSpec as P
+
+
+def collect(shard, axis, dim):
+    size, here, rows = (lax.axis_size(axis), lax.axis_index(axis), shard.shape[dim])
+    forward = [(i, (i + 1) % size) for i in range(size)]
+    downward = [(i, (i - 1) % size) for i in range(size)]
+    result = jnp.zeros((*shard.shape[:dim], size * rows, *shard.shape[dim + 1 :]), shard.dtype)
+    result = lax.dynamic_update_slice_in_dim(result, shard, here * rows, axis=dim)
+    from_left = from_right = shard
+    half = size // 2
+    for step in range(1, half + 1):
+        from_left = lax.ppermute(from_left, axis, forward)
+        result = lax.dynamic_update_slice_in_dim(
+            result, from_left, (here - step) % size * rows, axis=dim
+        )
+        if step < size - half:
+            from_right = lax.ppermute(from_right, axis, downward)
+            result = lax.dynamic_update_slice_in_dim(
+                result, from_right, (here + step) % size * rows, axis=dim
+            )
+    return result
 
 
 def expert_ffn(inputs, gate_mat, up_mat, down_mat):
@@ -29,11 +50,7 @@
     window = mamba_in.reshape(token_count, width)
     channels = in_weight.shape[1]
     taps = conv_kernel.shape[0]
-    summed_proj = jnp.dot(
-        window,
-        lax.all_gather(in_weight, "dp", axis=0, tiled=True),
-        preferred_element_type=jnp.float32,
-    )
+    summed_proj = jnp.dot(window, collect(in_weight, "dp", 0), preferred_element_type=jnp.float32)
     projected = summed_proj.astype(jnp.bfloat16)
     extended = jnp.concatenate([conv_state[0], projected], axis=0)
     summed = jnp.zeros((token_count, channels), jnp.float32) + conv_bias[None, :]

time: 354 us -> 366 us (1.034)
  local copies, waits for them, and re-layouts: 1.77 us -> 27.7 us
  waiting for transfers between devices: 234 us -> 211 us
  starting transfers between devices: 3.77 us -> 14.6 us
    ppermute x0 -> x7, waiting for transfers between devices: none -> 211 us  [the longest x4 206 us: collect(): from_left = lax.ppermute(from_left, axis, forward)]
    all_gather x1 -> x0, waiting for transfers between devices: 134 us -> none  [body(): lax.all_gather(in_weight, 'dp', axis=0, tiled=True)]
    reduce_scatter x1, waiting for transfers between devices: 88.7 us -> 0.01 us  [body(): shares = lax.psum_scatter(partials, 'dp', scatter_dimension=2, tiled=True)]
    dynamic_update_slice x0 -> x8, local copies, waits for them, and re-layouts: none -> 18.6 us  [the longest x4 9.32 us: collect(): lax.dynamic_update_slice_in_dim(result, from_left, (here - step) % size *...]
    ppermute x0 -> x7, starting transfers between devices: none -> 11.1 us  [the longest x3 11 us: collect(): from_right = lax.ppermute(from_right, axis, downward)]
    all_to_all x1, waiting for transfers between devices: 9.86 us -> 0.01 us  [body(): lax.all_to_all(shares, 'expert', split_axis=0, concat_axis=0, tiled=True)]
    broadcast_in_dim x0 -> x1, local copies, waits for them, and re-layouts: none -> 6.01 us  [collect(): jnp.zeros((*shard.shape[:dim], size * rows, *shard.shape[dim + 1:]), shar...]
  transfers between devices with their start and end apart: 3 -> 9, of which waited for: 3 -> 5; matrix products, arithmetic and copies ran while one was open for 1% -> 10% of each run, Pallas kernels for 0% -> 0%
where the time goes in v1:
time: 366 us
  waiting for transfers between devices  211 us (58%)
  blocking collectives  53.1 us (15%)
  matrix products  40.3 us (11%)
  local copies, waits for them, and re-layouts  27.7 us (8%)
  starting transfers between devices  14.6 us (4%)
  between operations  14.2 us (4%)
  other arithmetic  4.45 us (1%)
    ppermute x4, waiting for transfers between devices, collect(): from_left = lax.ppermute(from_left, axis, forward)  206 us
    all_to_all x1, blocking collectives, body(): lax.all_to_all(send_buffer, 'expert', split_axis=0, concat_axis=0, tiled=...  53.1 us
    ppermute x3, starting transfers between devices, collect(): from_right = lax.ppermute(from_right, axis, downward)  11 us
    dot_general x1, matrix products, expert_ffn(): up_val = jnp.dot(inputs, up_mat, preferred_element_type=jnp.float32)  10.4 us
    dynamic_update_slice x4, local copies, waits for them, and re-layouts, collect(): lax.dynamic_update_slice_in_dim(result, from_left, (here - step) % size *...  9.32 us
    dot_general x1, matrix products, expert_ffn(): return jnp.dot(hidden, down_mat, preferred_element_type=jnp.float32)  8.81 us
    dot_general x1, matrix products, expert_ffn(): gate_val = jnp.dot(inputs, gate_mat, preferred_element_type=jnp.float32)  8.35 us
    dot_general x1, matrix products, body(): jnp.dot(window, collect(in_weight, 'dp', 0), preferred_element_type=jnp.f...  8.26 us
  transfers between devices with their start and end apart: 9, of which 5 were waited for; matrix products, arithmetic and copies ran while one was open for 10% of the time, Pallas kernels for 0%

profile of v1, /device:TPU:0, one launch (start us, length us, event | category | flops | bytes accessed | tf_op | source)
XLA Modules:
  0.0 365.9 jit_solution(10384546399797475225)
XLA Ops:
  7.2 0.0 copy-start
  7.2 0.0 reduce-scatter.2.cloned.1.call-start
  7.2 0.9 copy.39
  8.2 0.1 eq.94
  8.3 0.1 eq.90
  8.4 1.2 reduce-window.6
  9.7 0.1 slice.56
  9.7 0.1 copy.41
  9.9 0.1 copy.42
  10.0 0.1 add_bitcast_fusion
  10.1 0.1 reshape.49
  10.2 0.1 copy.43
  10.3 0.7 multiply_add_fusion
  11.0 2.6 convolution_convert_fusion
  13.6 53.1 %all_to_all.10 = bf16[4,128,4096]{2,1,0:T(8,128)(2,1)S(1)} all-to-all(bf16[4,128,4096]{2,1,0:T(8,128)(2,1)S(1)} %bitcast.64), channel_id=1, replica_groups=mesh['dp'=8,'expert'=4] {'expert'}, dimensions={0} | all-to-all | bytes 8388608 | tf_op jit(solution)/shard_map/all_to_all | solution.py:87
  66.7 8.3 %fusion.4 = f32[512,1536]{1,0:T(8,128)} fusion(bf16[512,4096]{1,0:T(8,128)(2,1)S(1)} %bitcast.65, bf16[1,4096,1536]{2,1,0:T(8,128)(2,1)S(1)} %copy-done.10), kind=kOutput, calls=%fused_computation.4 | convolution fusion | flops 6442450944 | bytes 19922944 | tf_op jit(solution)/shard_map/dot_general | solution.py:29
  75.1 10.4 %fusion.9 = bf16[512,1536]{1,0:T(8,128)(2,1)S(1)} fusion(bf16[512,4096]{1,0:T(8,128)(2,1)S(1)} %bitcast.66, bf16[1,4096,1536]{2,1,0:T(8,128)(2,1)} %param.20, f32[512,1536]{1,0:T(8,128)} %fusion.4), kind=kOutput, calls=%fused_computation.8 | convolution fusion | flops 6447169536 | bytes 21495808 | tf_op jit(solution)/shard_map/dot_general | solution.py:30
  85.6 8.8 %fusion = f32[4,128,4096]{2,1,0:T(8,128)} fusion(bf16[4,128,1536]{2,1,0:T(8,128)(2,1)S(1)} %bitcast.77, bf16[1,1536,4096]{2,1,0:T(8,128)(2,1)S(1)} %bitcast.76), kind=kOutput, calls=%fused_computation | convolution fusion | flops 6442450944 | bytes 22544384 | tf_op jit(solution)/shard_map/dot_general | solution.py:32
  94.4 0.0 reduce-scatter.2.cloned.1.call-update
  94.4 0.1 collective-permute-start
  94.5 3.5 collective-permute-start.1
  98.0 82.2 %collective-permute-done = bf16[512,2048]{1,0:T(8,128)(2,1)S(1)} collective-permute-done((bf16[512,2048]{1,0:T(8,128)(2,1)}, bf16[512,2048]{1,0:T(8,128)(2,1)S(1)}, u32[]{:S(2)}, u32[]{:S(2)}) %collective-permute-start) | collective-permute-done | bytes 2097184 | tf_op jit(solution)/shard_map/ppermute | solution.py:16
  180.2 1.3 copy-done.3
  181.5 0.0 collective-permute-start.2
  181.5 5.6 %collective-permute-done.1 = bf16[512,2048]{1,0:T(8,128)(2,1)} collective-permute-done((bf16[512,2048]{1,0:T(8,128)(2,1)}, bf16[512,2048]{1,0:T(8,128)(2,1)}, u32[]{:S(2)}, u32[]{:S(2)}) %collective-permute-start.1) | collective-permute-done | bytes 2097184 | tf_op jit(solution)/shard_map/ppermute | solution.py:21
  187.2 3.7 %collective-permute-start.3 = (bf16[512,2048]{1,0:T(8,128)(2,1)}, bf16[512,2048]{1,0:T(8,128)(2,1)}, u32[]{:S(2)}, u32[]{:S(2)}) collective-permute-start(bf16[512,2048]{1,0:T(8,128)(2,1)} %collective-permute-done.1), channel_id=1, source_target_pairs={{0,28},{4,0},{8,4},{12,8},{16,12},{20,16},{24,20},{28,24},{1,29},{... | collective-permute-start | bytes 6291464 | tf_op jit(solution)/shard_map/ppermute | solution.py:21
  190.9 75.8 %collective-permute-done.2 = bf16[512,2048]{1,0:T(8,128)(2,1)} collective-permute-done((bf16[512,2048]{1,0:T(8,128)(2,1)S(1)}, bf16[512,2048]{1,0:T(8,128)(2,1)}, u32[]{:S(2)}, u32[]{:S(2)}) %collective-permute-start.2) | collective-permute-done | bytes 2097184 | tf_op jit(solution)/shard_map/ppermute | solution.py:16
  266.7 0.0 collective-permute-start.4
  266.8 0.4 fusion.34
  267.2 0.0 copy-start.2
  267.2 3.8 %collective-permute-start.5 = (bf16[512,2048]{1,0:T(8,128)(2,1)}, bf16[512,2048]{1,0:T(8,128)(2,1)S(1)}, u32[]{:S(2)}, u32[]{:S(2)}) collective-permute-start(bf16[512,2048]{1,0:T(8,128)(2,1)} %collective-permute-done.3), channel_id=1, source_target_pairs={{0,28},{4,0},{8,4},{12,8},{16,12},{20,16},{24,20},{28,24},{1,29},{... | collective-permute-start | bytes 6291464 | tf_op jit(solution)/shard_map/ppermute | solution.py:21
  271.0 6.0 %broadcast_in_dim.2 = bf16[4096,2048]{1,0:T(8,128)(2,1)} broadcast(bf16[]{:T(256)} %constant.64.clone.1), dimensions={} | broadcast | bytes 16777218 | tf_op jit(solution)/shard_map/broadcast_in_dim | solution.py:11
  277.0 1.5 constant_dynamic-update-slice_fusion.7
  278.5 36.0 %collective-permute-done.4 = bf16[512,2048]{1,0:T(8,128)(2,1)} collective-permute-done((bf16[512,2048]{1,0:T(8,128)(2,1)}, bf16[512,2048]{1,0:T(8,128)(2,1)}, u32[]{:S(2)}, u32[]{:S(2)}) %collective-permute-start.4) | collective-permute-done | bytes 2097184 | tf_op jit(solution)/shard_map/ppermute | solution.py:16
  314.5 1.4 constant_dynamic-update-slice_fusion.6
  315.9 3.2 constant_dynamic-update-slice_fusion.5
  319.1 3.2 constant_dynamic-update-slice_fusion.4
  322.3 3.2 constant_dynamic-update-slice_fusion.3
  325.4 3.2 constant_dynamic-update-slice_fusion.2
  328.6 1.5 constant_dynamic-update-slice_fusion.1
  330.1 11.8 %collective-permute-done.6 = bf16[512,2048]{1,0:T(8,128)(2,1)S(1)} collective-permute-done((bf16[512,2048]{1,0:T(8,128)(2,1)}, bf16[512,2048]{1,0:T(8,128)(2,1)S(1)}, u32[]{:S(2)}, u32[]{:S(2)}) %collective-permute-start.6) | collective-permute-done | bytes 2097184 | tf_op jit(solution)/shard_map/ppermute | solution.py:16
  341.9 1.5 constant_dynamic-update-slice_fusion
  343.4 3.5 all-to-all-start.1
  346.9 0.0 copy-start.7
  346.9 0.0 copy-start.9
  347.0 8.3 %fusion.12 = bf16[256,2048]{1,0:T(8,128)(2,1)S(1)} fusion(bf16[4096,2048]{1,0:T(8,128)(2,1)} %constant_dynamic-update-slice_fusion, bf16[1,256,4096]{2,1,0:T(8,128)(2,1)S(1)} %copy-done), kind=kOutput, calls=%fused_computation.10 | convolution fusion | flops 4295491584 | bytes 19922944 | tf_op jit(solution)/shard_map/dot_general | solution.py:53
  355.3 2.3 fusion.16
  357.6 1.4 convolution_convert_fusion.2
  (37 shorter events, 0.2 us)
Async XLA Ops:
  7.2 339.8 %copy-start = (bf16[1,256,4096]{2,1,0:T(8,128)(2,1)S(1)}, bf16[1,256,4096]{2,1,0:T(8,128)(2,1)}, u32[]{:S(2)}) copy-start(bf16[1,256,4096]{2,1,0:T(8,128)(2,1)} %param.11) | copy-start | bytes 6291460
  7.2 336.2 %reduce-scatter.2.cloned.1.call-start = ((), (), s32[]{:S(2)}) async-start(), calls=%async_computation.3 | async-start | bytes 9437184 | tf_op jit(solution)/shard_map/reduce_scatter | solution.py:91
  11.0 55.7 %copy-start.10 = (bf16[1,4096,1536]{2,1,0:T(8,128)(2,1)S(1)}, bf16[1,4096,1536]{2,1,0:T(8,128)(2,1)}, u32[]{:S(2)}) copy-start(bf16[1,4096,1536]{2,1,0:T(8,128)(2,1)} %param.19) | copy-start | bytes 37748740
  66.7 18.8 %slice-start = ((s8[12582912]{0:T(1024)(128)(4,1)}), s8[4194304]{0:T(1024)(128)(4,1)S(1)}, s32[]{:S(2)}) async-start(s8[12582912]{0:T(1024)(128)(4,1)} %bitcast.75), calls=%async_computation.4 | async-start | bytes 8388608
  66.7 18.8 %slice-start.1 = ((s8[12582912]{0:T(1024)(128)(4,1)}), s8[4194304]{0:T(1024)(128)(4,1)S(1)}, s32[]{:S(2)}) async-start(s8[12582912]{0:T(1024)(128)(4,1)} %bitcast.75), calls=%async_computation.5 | async-start | bytes 8388608
  75.1 10.5 %slice-start.2 = ((s8[12582912]{0:T(1024)(128)(4,1)}), s8[4194304]{0:T(1024)(128)(4,1)S(1)}, s32[]{:S(2)}) async-start(s8[12582912]{0:T(1024)(128)(4,1)} %bitcast.75), calls=%async_computation.6 | async-start | bytes 8388608
  94.4 172.4 %copy-start.1 = (bf16[128,4096]{1,0:T(8,128)(2,1)S(1)}, bf16[128,4096]{1,0:T(8,128)(2,1)}, u32[]{:S(2)}) copy-start(bf16[128,4096]{1,0:T(8,128)(2,1)} %param.16) | copy-start | bytes 3145732
  94.4 172.4 %copy-start.5 = (bf16[4096,4]{0,1:T(4,128)(2,1)S(1)}, bf16[4096,4]{0,1:T(4,128)(2,1)}, u32[]{:S(2)}) copy-start(bf16[4096,4]{0,1:T(4,128)(2,1)} %param.17) | copy-start | bytes 98308
  94.4 172.8 %copy-start.8 = (s32[128,2]{0,1:T(2,128)S(1)}, s32[128,2]{0,1:T(2,128)}, u32[]{:S(2)}) copy-start(s32[128,2]{0,1:T(2,128)} %param.18) | copy-start | bytes 3076
  94.4 85.8 %collective-permute-start = (bf16[512,2048]{1,0:T(8,128)(2,1)}, bf16[512,2048]{1,0:T(8,128)(2,1)S(1)}, u32[]{:S(2)}, u32[]{:S(2)}) collective-permute-start(bf16[512,2048]{1,0:T(8,128)(2,1)} %param.13), channel_id=1, source_target_pairs={{0,4},{4,8},{8,12},{12,16},{16,20},{20,24},{24,28},{28,0},{1,5},{5... | collective-permute-start | bytes 6291464 | tf_op jit(solution)/shard_map/ppermute | solution.py:16
  94.5 92.7 %collective-permute-start.1 = (bf16[512,2048]{1,0:T(8,128)(2,1)}, bf16[512,2048]{1,0:T(8,128)(2,1)}, u32[]{:S(2)}, u32[]{:S(2)}) collective-permute-start(bf16[512,2048]{1,0:T(8,128)(2,1)} %param.13), channel_id=1, source_target_pairs={{0,28},{4,0},{8,4},{12,8},{16,12},{20,16},{24,20},{28,24},{1,29},{... | collective-permute-start | bytes 6291464 | tf_op jit(solution)/shard_map/ppermute | solution.py:21
  180.2 1.3 copy-start.3
  181.5 85.2 %collective-permute-start.2 = (bf16[512,2048]{1,0:T(8,128)(2,1)S(1)}, bf16[512,2048]{1,0:T(8,128)(2,1)}, u32[]{:S(2)}, u32[]{:S(2)}) collective-permute-start(bf16[512,2048]{1,0:T(8,128)(2,1)S(1)} %collective-permute-done), channel_id=1, source_target_pairs={{0,4},{4,8},{8,12},{12,16},{16,20},{20,24},{24,28},{28,0},{1,5},{5... | collective-permute-start | bytes 6291464 | tf_op jit(solution)/shard_map/ppermute | solution.py:16
  187.2 80.0 %collective-permute-start.3 = (bf16[512,2048]{1,0:T(8,128)(2,1)}, bf16[512,2048]{1,0:T(8,128)(2,1)}, u32[]{:S(2)}, u32[]{:S(2)}) collective-permute-start(bf16[512,2048]{1,0:T(8,128)(2,1)} %collective-permute-done.1), channel_id=1, source_target_pairs={{0,28},{4,0},{8,4},{12,8},{16,12},{20,16},{24,20},{28,24},{1,29},{... | collective-permute-start | bytes 6291464 | tf_op jit(solution)/shard_map/ppermute | solution.py:21
  266.7 47.7 %collective-permute-start.4 = (bf16[512,2048]{1,0:T(8,128)(2,1)}, bf16[512,2048]{1,0:T(8,128)(2,1)}, u32[]{:S(2)}, u32[]{:S(2)}) collective-permute-start(bf16[512,2048]{1,0:T(8,128)(2,1)} %collective-permute-done.2), channel_id=1, source_target_pairs={{0,4},{4,8},{8,12},{12,16},{16,20},{20,24},{24,28},{28,0},{1,5},{5... | collective-permute-start | bytes 6291464 | tf_op jit(solution)/shard_map/ppermute | solution.py:16
  267.2 9.8 %copy-start.2 = (bf16[512,2048]{1,0:T(8,128)(2,1)S(1)}, bf16[512,2048]{1,0:T(8,128)(2,1)}, u32[]{:S(2)}) copy-start(bf16[512,2048]{1,0:T(8,128)(2,1)} %param.13) | copy-start | bytes 6291460
  267.2 61.4 %collective-permute-start.5 = (bf16[512,2048]{1,0:T(8,128)(2,1)}, bf16[512,2048]{1,0:T(8,128)(2,1)S(1)}, u32[]{:S(2)}, u32[]{:S(2)}) collective-permute-start(bf16[512,2048]{1,0:T(8,128)(2,1)} %collective-permute-done.3), channel_id=1, source_target_pairs={{0,28},{4,0},{8,4},{12,8},{16,12},{20,16},{24,20},{28,24},{1,29},{... | collective-permute-start | bytes 6291464 | tf_op jit(solution)/shard_map/ppermute | solution.py:21
  277.0 37.4 %copy-start.6 = (f32[4,2048]{1,0:T(4,128)S(1)}, f32[4,2048]{1,0:T(4,128)}, u32[]{:S(2)}) copy-start(f32[4,2048]{1,0:T(4,128)} %param.14) | copy-start | bytes 98308
  277.0 37.5 %copy-start.4 = (bf16[512,2048]{1,0:T(8,128)(2,1)S(1)}, bf16[512,2048]{1,0:T(8,128)(2,1)}, u32[]{:S(2)}) copy-start(bf16[512,2048]{1,0:T(8,128)(2,1)} %copy-done.3) | copy-start | bytes 6291460
  314.4 27.5 %collective-permute-start.6 = (bf16[512,2048]{1,0:T(8,128)(2,1)}, bf16[512,2048]{1,0:T(8,128)(2,1)S(1)}, u32[]{:S(2)}, u32[]{:S(2)}) collective-permute-start(bf16[512,2048]{1,0:T(8,128)(2,1)} %collective-permute-done.4), channel_id=1, source_target_pairs={{0,4},{4,8},{8,12},{12,16},{16,20},{20,24},{24,28},{28,0},{1,5},{5... | collective-permute-start | bytes 6291464 | tf_op jit(solution)/shard_map/ppermute | solution.py:16
  343.4 14.2 %all-to-all-start.1 = ((f32[4,128,512]{2,1,0:T(8,128)}), f32[4,128,512]{2,1,0:T(8,128)S(1)}, u32[]{:S(2)}, u32[]{:S(2)}) async-start(f32[4,128,512]{2,1,0:T(8,128)} %reduce-scatter.2.cloned.1.call-done), calls=%async_computation.2 | async-start | bytes 2097152 | tf_op jit(solution)/shard_map/all_to_all | solution.py:92
  346.9 8.3 %copy-start.7 = (bf16[1,3,2048]{2,1,0:T(4,128)(2,1)S(1)}, bf16[1,3,2048]{2,1,0:T(4,128)(2,1)}, u32[]{:S(2)}) copy-start(bf16[1,3,2048]{2,1,0:T(4,128)(2,1)} %param.12) | copy-start | bytes 36868
  346.9 8.3 %copy-start.9 = (f32[2048]{0:T(1024)S(1)}, f32[2048]{0:T(1024)}, u32[]{:S(2)}) copy-start(f32[2048]{0:T(1024)} %param.15) | copy-start | bytes 24580
Sparse Core Ops, SparseCore 0:
  94.5 164.9 reduce-scatter.1
